TPU v7x, 32 devices: a whole 2x2x4 slice. The times are simulated.
32 devices in a mesh: vox: 16 (over z, x, core), subj: 2 (over y).
Axes of the slice: x: 2, y: 2, z: 4, core: 2. Of those that a mesh axis runs over, the one named last changes fastest.
Arguments:
- series: bfloat16 [8, 4096, 512], P('subj', 'vox'), may hold values from -6 to 6
- live_mask: int32 [4096], P('vox'), may hold values from 0 to 1, as said below
- neighbours: int32 [4096, 13], P('vox'), may hold values from -1 to 510, as said below
- start_vectors: float32 [4096, 64], P('vox'), may hold values from -60 to 60
Outputs:
- embedding: float32 [4096, 64], P('vox')
Inputs may be any that keep to these rules, and one draw needn't show every extreme that they name: `live_mask`: within each aligned block of 128 voxel slots the live slots are a leading run of 1 to 128 slots. `neighbours`: slot n of voxel i names voxel (i // 256 - 1) * 256 + n, which is live and lies before i; the entries of a row are distinct or -1; rows of dead voxels are all -1; rows of the first 256 voxels name no slot under 256.
All inputs are finite; a program needn't handle non-finite values.
Results may differ from a plain program's by a relative error of at most 0.0024.
Values may be sent and summed in bfloat16 or wider, within the bound.
No kernel may reach another device: no remote copies, remote signals or barrier semaphores. Data moves between devices by JAX's collectives and lax.ppermute only.
A program may use at most 64 MiB of HBM per device.

v0:
```python
import math

import jax
import jax.numpy as jnp
from jax import lax
from jax.sharding import PartitionSpec as P

ITERS = 3


def shifted(shard, axis, by):
    count = lax.axis_size(axis)
    pairs = [(i, i + by) for i in range(count) if 0 <= i + by < count]
    return lax.ppermute(shard, axis, pairs)


def as_sent(shard):
    return jax.tree.map(lambda a: a.astype(jnp.bfloat16) if a.dtype == jnp.float32 else a, shard)


def standard(block):
    values = block.astype(jnp.float32)
    center = values - jnp.mean(values, axis=-1, keepdims=True)
    spread = jnp.mean(center * center, axis=-1, keepdims=True)
    return (center * lax.rsqrt(spread + 1e-05)).astype(jnp.bfloat16)


def orthonormal(images):
    gram_matrix = jnp.dot(images.T, images, precision=lax.Precision.HIGHEST)
    gram_matrix = lax.psum(gram_matrix, "vox")
    factor = jnp.linalg.cholesky(gram_matrix)
    return lax.linalg.triangular_solve(
        factor, images, left_side=False, lower=True, transpose_a=True
    )


def dense_graph(weight, slots, columns_total):
    column_ids = jnp.arange(columns_total, dtype=jnp.int32)
    matrix = jnp.zeros((weight.shape[0], columns_total), jnp.float32)
    for offset in range(weight.shape[1]):
        hits = (slots[:, offset][:, None] == column_ids[None, :]).astype(jnp.float32)
        matrix = matrix + weight[:, offset][:, None] * hits
    return matrix


def product(left, right):
    return jnp.dot(left, right, precision=lax.Precision.HIGHEST)


def on_device(series, live_mask, neighbours, start_vectors):
    voxels_here = series.shape[1]
    frames = series.shape[2]
    subjects = series.shape[0] * lax.axis_size("subj")
    scale_factor = 0.5 / math.sqrt(frames * subjects)
    zscored = standard(series)
    earlier = shifted(zscored, "vox", 1)
    window = jnp.concatenate([earlier, zscored], axis=1)
    present = neighbours >= 0
    safe_slots = jnp.maximum(neighbours, 0)
    columns = []
    for offset in range(neighbours.shape[1]):
        picked = jnp.take(window, safe_slots[:, offset], axis=1)
        columns.append(
            jnp.einsum("svf,svf->v", zscored, picked, preferred_element_type=jnp.float32)
        )
    partial_sums = jnp.stack(columns, axis=1)
    summed = lax.psum(partial_sums, "subj")
    weight = jnp.where(present, jnp.exp(scale_factor * summed), 0.0)
    living = live_mask.astype(jnp.float32)
    local_graph = dense_graph(weight, neighbours, 2 * voxels_here)
    owed = jnp.sum(local_graph, axis=0)
    received = shifted(owed[:voxels_here], "vox", -1)
    degree = 1.0 + jnp.sum(weight, axis=1) + owed[voxels_here:] + received
    scaling = living * lax.rsqrt(degree)
    vectors = living[:, None] * start_vectors
    for repeat in range(ITERS):
        scaled = scaling[:, None] * vectors
        earlier_rows = shifted(as_sent(scaled), "vox", 1).astype(scaled.dtype)
        window_rows = jnp.concatenate([earlier_rows, scaled], axis=0)
        forward = product(local_graph, window_rows)
        returns = product(local_graph.T, scaled)
        arrived = shifted(as_sent(returns[:voxels_here]), "vox", -1)
        images = 0.5 * (
            vectors + scaling[:, None] * (scaled + forward + returns[voxels_here:] + arrived)
        )
        vectors = orthonormal(images)
    return vectors


def solution(mesh):
    placed = (P("subj", "vox", None), P("vox"), P("vox", None), P("vox", None))
    return jax.shard_map(
        on_device, mesh=mesh, in_specs=placed, out_specs=P("vox", None), check_vma=False
    )
```

profile of v0, /device:TPU:0, one launch (start us, length us, event | category | flops | bytes accessed | tf_op | source)
XLA Modules:
  0.0 326.7 jit_solution(9285607745963571878)
XLA Ops:
  0.0 2.1 convert_reduce_fusion
  2.2 1.2 fusion.2
  3.4 1.6 fusion.3
  5.0 2.6 collective-permute-start
  7.8 0.5 compare_and_fusion.8
  8.6 0.5 compare_and_fusion.2
  9.1 0.5 compare_and_fusion.4
  9.6 0.6 compare_and_fusion.6
  10.2 1.4 pad_maximum_fusion
  11.6 2.5 gather_fusion.3
  14.0 2.5 gather_fusion.2
  16.5 2.5 gather_fusion.1
  19.0 2.5 gather_fusion
  21.5 2.5 gather_fusion.12
  24.0 2.5 gather_fusion.11
  26.5 2.5 gather_fusion.10
  28.9 2.4 gather_fusion.9
  31.4 2.5 gather_fusion.8
  33.9 2.5 gather_fusion.7
  36.4 2.7 gather_fusion.6
  39.1 2.5 gather_fusion.5
  41.6 2.5 gather_fusion.4
  44.1 9.5 %fusion.7 = (f32[256]{0:T(256)S(1)}, f32[256]{0:T(256)S(1)}, f32[256]{0:T(256)S(1)}, f32[256]{0:T(256)S(1)}) fusion(bf16[256,4,512]{2,1,0:T(4,128)(2,1)} %gather_fusion.3, pred[256]{0:T(512)(128)(4,1)S(1)} %get-tuple-element.72, bf16[256,4,512]{2,1,0:T(4,128)(2,1)} %gather_fusion.2, pred[256]{0:T(512)(128)(4,1)S(1)} %get-tuple-element.73, ...), kind=kLoop, calls=%fused_computation.35 | loop fusion | flops 11009024 | bytes 5256192 | tf_op jit(solution)/shard_map/svf,svf->v/dot_general | solution.py:64
  53.7 14.7 %fusion.16 = (f32[256]{0:T(256)S(1)}, f32[256]{0:T(256)S(1)}, f32[256]{0:T(256)S(1)}, f32[256]{0:T(256)S(1)}, f32[256]{0:T(256)S(1)}, /*index=5*/f32[256]{0:T(25...) fusion(bf16[256,4,512]{2,1,0:T(4,128)(2,1)S(1)} %copy-done.1, pred[256]{0:T(512)(128)(4,1)S(1)} %get-tuple-element.76, ...), kind=kLoop, calls=%fused_computation.44 | loop fusion | flops 21493504 | bytes 10505472 | tf_op jit(solution)/shard_map/svf,svf->v/dot_general | solution.py:64
  68.5 9.0 %psum.28 = f32[256,13]{0,1:T(8,128)S(1)} all-reduce(f32[256,13]{0,1:T(8,128)S(1)} %stack.55), channel_id=1, replica_groups=mesh['vox'=16,'subj'=2] {'subj'}, use_global_device_ids=true, to_apply=%region_2.0 | all-reduce | flops 3328 | bytes 26624 | tf_op jit(solution)/shard_map/psum | solution.py:67
  77.5 1.0 fusion.61
  78.5 1.3 collective-permute-start.1
  79.8 9.8 %collective-permute-done.1 = f32[256]{0:T(256)S(1)} collective-permute-done((f32[256]{0:T(256)S(1)}, f32[256]{0:T(256)S(1)}, u32[]{:S(2)}, u32[]{:S(2)}) %collective-permute-start.1) | collective-permute-done | bytes 1056 | tf_op jit(solution)/shard_map/ppermute | solution.py:14
  89.7 7.0 %collective-permute-start.2 = (bf16[256,64]{0,1:T(8,128)(2,1)S(1)}, bf16[256,64]{0,1:T(8,128)(2,1)S(1)}, u32[]{:S(2)}, u32[]{:S(2)}) collective-permute-start(bf16[256,64]{0,1:T(8,128)(2,1)S(1)} %get-tuple-element.25), channel_id=1, source_target_pairs={{0,2},{2,4},{4,6},{6,8},{8,10},{10,12},{12,14},{14,16},{16,18},{18... | collective-permute-start | bytes 98312 | tf_op jit(solution)/shard_map/ppermute | solution.py:14
  96.7 0.5 fusion.65
  97.2 1.3 collective-permute-start.3
  98.5 1.8 collective-permute-done.3
  100.3 0.6 fusion.31
  100.9 0.2 fusion.66
  101.1 60.5 %psum.29 = f32[64,64]{0,1:T(8,128)S(1)} all-reduce(f32[64,64]{0,1:T(8,128)S(1)} %fusion.66), channel_id=1, replica_groups=mesh['vox'=16,'subj'=2] {'vox'}, use_global_device_ids=true, to_apply=%region_5.7 | all-reduce | flops 4096 | bytes 32768 | tf_op jit(solution)/shard_map/psum | solution.py:30
  161.7 5.8 %cholesky.59 = f32[64,64]{1,0:T(8,128)S(1)} custom-call(f32[64,64]{1,0:T(8,128)S(1)} %fusion.49), custom_call_target="Cholesky" | custom-call | tf_op jit(solution)/shard_map/jit(cholesky)/cholesky | solution.py:31
  167.6 0.6 compare_reduce_fusion.2
  168.2 0.7 fusion.41
  168.9 4.9 %custom-call.7 = f32[1,64,64]{1,2,0:T(8,128)S(1)} custom-call(f32[1,64,64]{2,1,0:T(8,128)S(1)} %fusion.41), custom_call_target="InvertDiagBlocksLowerTriangular" | custom-call | tf_op jit(solution)/shard_map/triangular_solve/custom-call.0 | solution.py:32
  173.8 0.3 fusion.58
  174.1 1.3 collective-permute-start.4
  175.4 0.5 fusion.67
  175.8 1.3 collective-permute-start.5
  177.2 1.8 collective-permute-done.5
  178.9 0.6 fusion.26
  179.6 0.2 fusion.68
  179.8 57.9 %psum.30 = f32[64,64]{0,1:T(8,128)S(1)} all-reduce(f32[64,64]{0,1:T(8,128)S(1)} %fusion.68), channel_id=1, replica_groups=mesh['vox'=16,'subj'=2] {'vox'}, use_global_device_ids=true, to_apply=%region_8.12 | all-reduce | flops 4096 | bytes 32768 | tf_op jit(solution)/shard_map/psum | solution.py:30
  237.8 5.8 %cholesky.70 = f32[64,64]{1,0:T(8,128)S(1)} custom-call(f32[64,64]{1,0:T(8,128)S(1)} %fusion.47), custom_call_target="Cholesky" | custom-call | tf_op jit(solution)/shard_map/jit(cholesky)/cholesky | solution.py:31
  243.6 0.6 compare_reduce_fusion.1
  244.3 0.7 fusion.42
  244.9 4.9 %custom-call.8 = f32[1,64,64]{1,2,0:T(8,128)S(1)} custom-call(f32[1,64,64]{2,1,0:T(8,128)S(1)} %fusion.42), custom_call_target="InvertDiagBlocksLowerTriangular" | custom-call | tf_op jit(solution)/shard_map/triangular_solve/custom-call.0 | solution.py:32
  249.8 0.3 fusion.57
  250.1 1.3 collective-permute-start.6
  251.4 0.5 fusion.69
  251.9 1.3 collective-permute-start.7
  253.2 1.8 collective-permute-done.7
  255.0 0.6 fusion.21
  255.6 0.2 fusion.70
  255.8 57.7 %psum.31 = f32[64,64]{0,1:T(8,128)S(1)} all-reduce(f32[64,64]{0,1:T(8,128)S(1)} %fusion.70), channel_id=1, replica_groups=mesh['vox'=16,'subj'=2] {'vox'}, use_global_device_ids=true, to_apply=%region_9.13 | all-reduce | flops 4096 | bytes 32768 | tf_op jit(solution)/shard_map/psum | solution.py:30
  313.7 5.8 %cholesky.81 = f32[64,64]{1,0:T(8,128)S(1)} custom-call(f32[64,64]{1,0:T(8,128)S(1)} %fusion.45), custom_call_target="Cholesky" | custom-call | tf_op jit(solution)/shard_map/jit(cholesky)/cholesky | solution.py:31
  319.5 0.6 compare_reduce_fusion
  320.2 0.7 fusion.43
  320.9 4.9 %custom-call.9 = f32[1,64,64]{1,2,0:T(8,128)S(1)} custom-call(f32[1,64,64]{2,1,0:T(8,128)S(1)} %fusion.43), custom_call_target="InvertDiagBlocksLowerTriangular" | custom-call | tf_op jit(solution)/shard_map/triangular_solve/custom-call.0 | solution.py:32
  325.7 0.9 convolution_bitcast_fusion
  (92 shorter events, 0.8 us)
Async XLA Ops:
  0.0 2.2 copy-start
  2.1 5.5 %copy-start.7 = (s32[256,13]{0,1:T(8,128)S(1)}, s32[256,13]{0,1:T(8,128)}, u32[]{:S(2)}) copy-start(s32[256,13]{0,1:T(8,128)} %param.11) | copy-start | bytes 39940
  5.0 5.2 %collective-permute-start = (bf16[4,256,512]{2,0,1:T(4,128)(2,1)S(1)}, bf16[4,256,512]{2,0,1:T(4,128)(2,1)S(1)}, u32[]{:S(2)}, u32[]{:S(2)}) collective-permute-start(bf16[4,256,512]{2,0,1:T(4,128)(2,1)S(1)} %fusion.3), channel_id=1, source_target_pairs={{0,2},{2,4},{4,6},{6,8},{8,10},{10,12},{12,14},{14,16},{16,18},{18... | collective-permute-start | bytes 3145736 | tf_op jit(solution)/shard_map/ppermute | solution.py:14
  44.0 9.6 %copy-start.1 = (bf16[256,4,512]{2,1,0:T(4,128)(2,1)S(1)}, bf16[256,4,512]{2,1,0:T(4,128)(2,1)}, u32[]{:S(2)}) copy-start(bf16[256,4,512]{2,1,0:T(4,128)(2,1)} %gather_fusion.12) | copy-start | bytes 3145732
  44.0 9.6 %copy-start.2 = (bf16[256,4,512]{2,1,0:T(4,128)(2,1)S(1)}, bf16[256,4,512]{2,1,0:T(4,128)(2,1)}, u32[]{:S(2)}) copy-start(bf16[256,4,512]{2,1,0:T(4,128)(2,1)} %gather_fusion.11) | copy-start | bytes 3145732
  44.0 9.6 %copy-start.3 = (bf16[256,4,512]{2,1,0:T(4,128)(2,1)S(1)}, bf16[256,4,512]{2,1,0:T(4,128)(2,1)}, u32[]{:S(2)}) copy-start(bf16[256,4,512]{2,1,0:T(4,128)(2,1)} %gather_fusion.10) | copy-start | bytes 3145732
  44.0 9.6 %copy-start.4 = (bf16[256,4,512]{2,1,0:T(4,128)(2,1)S(1)}, bf16[256,4,512]{2,1,0:T(4,128)(2,1)}, u32[]{:S(2)}) copy-start(bf16[256,4,512]{2,1,0:T(4,128)(2,1)} %gather_fusion.9) | copy-start | bytes 3145732
  44.0 9.6 %copy-start.5 = (bf16[256,4,512]{2,1,0:T(4,128)(2,1)S(1)}, bf16[256,4,512]{2,1,0:T(4,128)(2,1)}, u32[]{:S(2)}) copy-start(bf16[256,4,512]{2,1,0:T(4,128)(2,1)} %gather_fusion.8) | copy-start | bytes 3145732
  44.0 9.6 %copy-start.9 = (pred[256]{0:T(512)(128)(4,1)S(1)}, pred[256]{0:T(512)(128)(4,1)}, u32[]{:S(2)}) copy-start(pred[256]{0:T(512)(128)(4,1)} %get-tuple-element.78) | copy-start | bytes 772
  44.0 9.6 %copy-start.10 = (pred[256]{0:T(512)(128)(4,1)S(1)}, pred[256]{0:T(512)(128)(4,1)}, u32[]{:S(2)}) copy-start(pred[256]{0:T(512)(128)(4,1)} %get-tuple-element.79) | copy-start | bytes 772
  44.1 9.6 %copy-start.11 = (pred[256]{0:T(512)(128)(4,1)S(1)}, pred[256]{0:T(512)(128)(4,1)}, u32[]{:S(2)}) copy-start(pred[256]{0:T(512)(128)(4,1)} %get-tuple-element.80) | copy-start | bytes 772
  44.1 9.6 %copy-start.12 = (pred[256]{0:T(512)(128)(4,1)S(1)}, pred[256]{0:T(512)(128)(4,1)}, u32[]{:S(2)}) copy-start(pred[256]{0:T(512)(128)(4,1)} %get-tuple-element.81) | copy-start | bytes 772
  44.1 9.6 %copy-start.13 = (pred[256]{0:T(512)(128)(4,1)S(1)}, pred[256]{0:T(512)(128)(4,1)}, u32[]{:S(2)}) copy-start(pred[256]{0:T(512)(128)(4,1)} %get-tuple-element.82) | copy-start | bytes 772
  44.1 9.6 %copy-start.14 = (pred[256]{0:T(512)(128)(4,1)S(1)}, pred[256]{0:T(512)(128)(4,1)}, u32[]{:S(2)}) copy-start(pred[256]{0:T(512)(128)(4,1)} %get-tuple-element.83) | copy-start | bytes 772
  44.1 9.6 %copy-start.15 = (pred[256]{0:T(512)(128)(4,1)S(1)}, pred[256]{0:T(512)(128)(4,1)}, u32[]{:S(2)}) copy-start(pred[256]{0:T(512)(128)(4,1)} %compare_and_fusion.8) | copy-start | bytes 772
  53.7 26.1 %copy-start.8 = (s32[256]{0:T(256)S(1)}, s32[256]{0:T(256)}, u32[]{:S(2)}) copy-start(s32[256]{0:T(256)} %param.10) | copy-start | bytes 3076
  53.7 35.9 %copy-start.6 = (f32[256,64]{0,1:T(8,128)S(1)}, f32[256,64]{0,1:T(8,128)}, u32[]{:S(2)}) copy-start(f32[256,64]{0,1:T(8,128)} %param.12) | copy-start | bytes 196612
  78.5 11.2 %collective-permute-start.1 = (f32[256]{0:T(256)S(1)}, f32[256]{0:T(256)S(1)}, u32[]{:S(2)}, u32[]{:S(2)}) collective-permute-start(f32[256]{0:T(256)S(1)} %slice.190), channel_id=1, source_target_pairs={{2,0},{4,2},{6,4},{8,6},{10,8},{12,10},{14,12},{16,14},{18,16},{20... | collective-permute-start | bytes 3080 | tf_op jit(solution)/shard_map/ppermute | solution.py:14
  89.7 8.8 %collective-permute-start.2 = (bf16[256,64]{0,1:T(8,128)(2,1)S(1)}, bf16[256,64]{0,1:T(8,128)(2,1)S(1)}, u32[]{:S(2)}, u32[]{:S(2)}) collective-permute-start(bf16[256,64]{0,1:T(8,128)(2,1)S(1)} %get-tuple-element.25), channel_id=1, source_target_pairs={{0,2},{2,4},{4,6},{6,8},{8,10},{10,12},{12,14},{14,16},{16,18},{18... | collective-permute-start | bytes 98312 | tf_op jit(solution)/shard_map/ppermute | solution.py:14
  97.2 3.1 collective-permute-start.3
  174.1 3.1 collective-permute-start.4
  175.8 3.1 collective-permute-start.5
  250.1 3.1 collective-permute-start.6
  251.9 3.1 collective-permute-start.7
where the time goes:
time: 327 us
  blocking collectives  185 us (57%)
  other arithmetic  70 us (21%)
  local copies, waits for them, and re-layouts  32.8 us (10%)
  starting transfers between devices  17.4 us (5%)
  waiting for transfers between devices  15.2 us (5%)
  matrix products  5.27 us (2%)
    psum x3, blocking collectives, orthonormal(): gram_matrix = lax.psum(gram_matrix, 'vox')  176 us
    gather x13, local copies, waits for them, and re-layouts, on_device(): picked = jnp.take(window, safe_slots[:, offset], axis=1)  32.4 us
    dot_general x2, other arithmetic, on_device(): jnp.einsum('svf,svf->v', zscored, picked, preferred_element_type=jnp.floa...  24.1 us
    another operation x9, other arithmetic, orthonormal(): factor = jnp.linalg.cholesky(gram_matrix)  19.6 us
    ppermute x8, starting transfers between devices, shifted(): return lax.ppermute(shard, axis, pairs)  17.4 us
    another operation x6, other arithmetic, orthonormal(): lax.linalg.triangular_solve(factor, images, left_side=False, lower=True,...  16.6 us
    ppermute x8, waiting for transfers between devices, shifted(): return lax.ppermute(shard, axis, pairs)  15.2 us
    psum x1, blocking collectives, on_device(): summed = lax.psum(partial_sums, 'subj')  8.99 us
  transfers between devices with their start and end apart: 8, of which 4 were waited for; matrix products, arithmetic and copies ran while one was open for 1% of the time, Pallas kernels for 0%

commit v1 on v0

--- a/solution.py
+++ b/solution.py
@@ -14,6 +14,27 @@
     return lax.ppermute(shard, axis, pairs)
 
 
+def exchanged(value, axis, distance):
+    count = lax.axis_size(axis)
+    return lax.ppermute(value, axis, [(i, i ^ distance) for i in range(count)])
+
+
+def summed_over(value, axis):
+    count = lax.axis_size(axis)
+    if count & (count - 1):
+        return lax.psum(value, axis)
+    stride = 1
+    while stride < count:
+        if stride > 1 and 4 * stride <= count:
+            first, second, third = (exchanged(value, axis, k * stride) for k in (1, 2, 3))
+            value = (value + first) + (second + third)
+            stride *= 4
+        else:
+            value = value + exchanged(value, axis, stride)
+            stride *= 2
+    return value
+
+
 def as_sent(shard):
     return jax.tree.map(lambda a: a.astype(jnp.bfloat16) if a.dtype == jnp.float32 else a, shard)
 
@@ -27,7 +48,7 @@
 
 def orthonormal(images):
     gram_matrix = jnp.dot(images.T, images, precision=lax.Precision.HIGHEST)
-    gram_matrix = lax.psum(gram_matrix, "vox")
+    gram_matrix = summed_over(gram_matrix, "vox")
     factor = jnp.linalg.cholesky(gram_matrix)
     return lax.linalg.triangular_solve(
         factor, images, left_side=False, lower=True, transpose_a=True

time: 327 us -> 204 us (0.62)
  blocking collectives: 185 us -> 8.99 us
  waiting for transfers between devices: 15.2 us -> 42.4 us
  starting transfers between devices: 17.4 us -> 42.8 us
    psum x3 -> x0, blocking collectives: 176 us -> none  [orthonormal(): gram_matrix = lax.psum(gram_matrix, 'vox')]
    ppermute x0 -> x15, starting transfers between devices: none -> 25.2 us  [exchanged(): return lax.ppermute(value, axis, [(i, i ^ distance) for i in range(count)])]
    ppermute x0 -> x15, waiting for transfers between devices: none -> 25 us  [exchanged(): return lax.ppermute(value, axis, [(i, i ^ distance) for i in range(count)])]
  transfers between devices with their start and end apart: 8 -> 23, of which waited for: 4 -> 16; matrix products, arithmetic and copies ran while one was open for 1% -> 2% of each run, Pallas kernels for 0% -> 0%
where the time goes in v1:
time: 204 us; the launch traced here: 203 us
  other arithmetic  70.1 us (34%)
  starting transfers between devices  42.8 us (21%)
  waiting for transfers between devices  42.4 us (21%)
  local copies, waits for them, and re-layouts  32.8 us (16%)
  blocking collectives  8.99 us (4%)
  matrix products  5.26 us (3%)
    gather x13, local copies, waits for them, and re-layouts, on_device(): picked = jnp.take(window, safe_slots[:, offset], axis=1)  32.3 us
    ppermute x15, starting transfers between devices, exchanged(): return lax.ppermute(value, axis, [(i, i ^ distance) for i in range(count)])  25.2 us
    ppermute x15, waiting for transfers between devices, exchanged(): return lax.ppermute(value, axis, [(i, i ^ distance) for i in range(count)])  25 us
    dot_general x2, other arithmetic, on_device(): jnp.einsum('svf,svf->v', zscored, picked, preferred_element_type=jnp.floa...  24.1 us
    another operation x9, other arithmetic, orthonormal(): factor = jnp.linalg.cholesky(gram_matrix)  19.6 us
    ppermute x8, starting transfers between devices, shifted(): return lax.ppermute(shard, axis, pairs)  17.6 us
    ppermute x8, waiting for transfers between devices, shifted(): return lax.ppermute(shard, axis, pairs)  17.4 us
    another operation x6, other arithmetic, orthonormal(): lax.linalg.triangular_solve(factor, images, left_side=False, lower=True,...  16.6 us
  transfers between devices with their start and end apart: 23, of which 16 were waited for; matrix products, arithmetic and copies ran while one was open for 2% of the time, Pallas kernels for 0%

profile of v1, /device:TPU:0, one launch (start us, length us, event | category | flops | bytes accessed | tf_op | source)
XLA Modules:
  0.0 203.2 jit_solution(12058164480931716978)
XLA Ops:
  0.0 2.1 %convert_reduce_fusion = f32[4,256]{0,1:T(8,128)S(1)} fusion(bf16[4,256,512]{2,1,0:T(8,128)(2,1)} %param.9), kind=kLoop, calls=%fused_computation.27 | loop fusion | flops 1047552 | bytes 1052672 | tf_op jit(solution)/shard_map/reduce_sum | solution.py:44
  2.2 1.2 fusion.2
  3.4 1.6 fusion.3
  5.0 2.6 %collective-permute-start = (bf16[4,256,512]{2,0,1:T(4,128)(2,1)S(1)}, bf16[4,256,512]{2,0,1:T(4,128)(2,1)S(1)}, u32[]{:S(2)}, u32[]{:S(2)}) collective-permute-start(bf16[4,256,512]{2,0,1:T(4,128)(2,1)S(1)} %fusion.3), channel_id=1, source_target_pairs={{0,2},{2,4},{4,6},{6,8},{8,10},{10,12},{12,14},{14,16},{16,18},{18... | collective-permute-start | bytes 3145736 | tf_op jit(solution)/shard_map/ppermute | solution.py:14
  10.2 1.4 pad_maximum_fusion
  11.6 2.4 %gather_fusion.3 = bf16[256,4,512]{2,1,0:T(4,128)(2,1)} fusion(bf16[4,512,512]{2,0,1:T(4,128)(2,1)S(1)} %pad_maximum_fusion, s32[1024]{0:T(1024)S(1)} %pad_clamp_fusion.9), kind=kCustom, calls=%fused_computation.3.clone | custom fusion | bytes 2098176 | tf_op jit(solution)/shard_map/jit(_take)/gather | solution.py:83
  14.0 2.5 %gather_fusion.2 = bf16[256,4,512]{2,1,0:T(4,128)(2,1)} fusion(bf16[4,512,512]{2,0,1:T(4,128)(2,1)S(1)} %pad_maximum_fusion, s32[1024]{0:T(1024)S(1)} %pad_clamp_fusion.10), kind=kCustom, calls=%fused_computation.2.clone | custom fusion | bytes 2098176 | tf_op jit(solution)/shard_map/jit(_take)/gather | solution.py:83
  16.5 2.5 %gather_fusion.1 = bf16[256,4,512]{2,1,0:T(4,128)(2,1)} fusion(bf16[4,512,512]{2,0,1:T(4,128)(2,1)S(1)} %pad_maximum_fusion, s32[1024]{0:T(1024)S(1)} %pad_clamp_fusion.11), kind=kCustom, calls=%fused_computation.1.clone | custom fusion | bytes 2098176 | tf_op jit(solution)/shard_map/jit(_take)/gather | solution.py:83
  19.0 2.4 %gather_fusion = bf16[256,4,512]{2,1,0:T(4,128)(2,1)} fusion(bf16[4,512,512]{2,0,1:T(4,128)(2,1)S(1)} %pad_maximum_fusion, s32[1024]{0:T(1024)S(1)} %pad_clamp_fusion.12), kind=kCustom, calls=%fused_computation.clone | custom fusion | bytes 2098176 | tf_op jit(solution)/shard_map/jit(_take)/gather | solution.py:83
  21.4 2.5 %gather_fusion.12 = bf16[256,4,512]{2,1,0:T(4,128)(2,1)} fusion(bf16[4,512,512]{2,0,1:T(4,128)(2,1)S(1)} %pad_maximum_fusion, s32[1024]{0:T(1024)S(1)} %pad_clamp_fusion), kind=kCustom, calls=%fused_computation.12.clone | custom fusion | bytes 2098176 | tf_op jit(solution)/shard_map/jit(_take)/gather | solution.py:83
  24.0 2.4 %gather_fusion.11 = bf16[256,4,512]{2,1,0:T(4,128)(2,1)} fusion(bf16[4,512,512]{2,0,1:T(4,128)(2,1)S(1)} %pad_maximum_fusion, s32[1024]{0:T(1024)S(1)} %pad_clamp_fusion.1), kind=kCustom, calls=%fused_computation.11.clone | custom fusion | bytes 2098176 | tf_op jit(solution)/shard_map/jit(_take)/gather | solution.py:83
  26.4 2.4 %gather_fusion.10 = bf16[256,4,512]{2,1,0:T(4,128)(2,1)} fusion(bf16[4,512,512]{2,0,1:T(4,128)(2,1)S(1)} %pad_maximum_fusion, s32[1024]{0:T(1024)S(1)} %pad_clamp_fusion.2), kind=kCustom, calls=%fused_computation.10.clone | custom fusion | bytes 2098176 | tf_op jit(solution)/shard_map/jit(_take)/gather | solution.py:83
  28.9 2.4 %gather_fusion.9 = bf16[256,4,512]{2,1,0:T(4,128)(2,1)} fusion(bf16[4,512,512]{2,0,1:T(4,128)(2,1)S(1)} %pad_maximum_fusion, s32[1024]{0:T(1024)S(1)} %pad_clamp_fusion.3), kind=kCustom, calls=%fused_computation.9.clone | custom fusion | bytes 2098176 | tf_op jit(solution)/shard_map/jit(_take)/gather | solution.py:83
  31.3 2.5 %gather_fusion.8 = bf16[256,4,512]{2,1,0:T(4,128)(2,1)} fusion(bf16[4,512,512]{2,0,1:T(4,128)(2,1)S(1)} %pad_maximum_fusion, s32[1024]{0:T(1024)S(1)} %pad_clamp_fusion.4), kind=kCustom, calls=%fused_computation.8.clone | custom fusion | bytes 2098176 | tf_op jit(solution)/shard_map/jit(_take)/gather | solution.py:83
  33.8 2.5 %gather_fusion.7 = bf16[256,4,512]{2,1,0:T(4,128)(2,1)} fusion(bf16[4,512,512]{2,0,1:T(4,128)(2,1)S(1)} %pad_maximum_fusion, s32[1024]{0:T(1024)S(1)} %pad_clamp_fusion.5), kind=kCustom, calls=%fused_computation.7.clone | custom fusion | bytes 2098176 | tf_op jit(solution)/shard_map/jit(_take)/gather | solution.py:83
  36.3 2.7 %gather_fusion.6 = bf16[256,4,512]{2,1,0:T(4,128)(2,1)} fusion(bf16[4,512,512]{2,0,1:T(4,128)(2,1)S(1)} %pad_maximum_fusion, s32[1024]{0:T(1024)S(1)} %pad_clamp_fusion.6), kind=kCustom, calls=%fused_computation.6.clone | custom fusion | bytes 2098176 | tf_op jit(solution)/shard_map/jit(_take)/gather | solution.py:83
  39.0 2.5 %gather_fusion.5 = bf16[256,4,512]{2,1,0:T(4,128)(2,1)} fusion(bf16[4,512,512]{2,0,1:T(4,128)(2,1)S(1)} %pad_maximum_fusion, s32[1024]{0:T(1024)S(1)} %pad_clamp_fusion.7), kind=kCustom, calls=%fused_computation.5.clone | custom fusion | bytes 2098176 | tf_op jit(solution)/shard_map/jit(_take)/gather | solution.py:83
  41.5 2.5 %gather_fusion.4 = bf16[256,4,512]{2,1,0:T(4,128)(2,1)} fusion(bf16[4,512,512]{2,0,1:T(4,128)(2,1)S(1)} %pad_maximum_fusion, s32[1024]{0:T(1024)S(1)} %pad_clamp_fusion.8), kind=kCustom, calls=%fused_computation.4.clone | custom fusion | bytes 2098176 | tf_op jit(solution)/shard_map/jit(_take)/gather | solution.py:83
  44.0 9.5 %fusion.7 = (f32[256]{0:T(256)S(1)}, f32[256]{0:T(256)S(1)}, f32[256]{0:T(256)S(1)}, f32[256]{0:T(256)S(1)}) fusion(bf16[256,4,512]{2,1,0:T(4,128)(2,1)} %gather_fusion.3, pred[256]{0:T(512)(128)(4,1)S(1)} %get-tuple-element.72, bf16[256,4,512]{2,1,0:T(4,128)(2,1)} %gather_fusion.2, pred[256]{0:T(512)(128)(4,1)S(1)} %get-tuple-element.73, ...), kind=kLoop, calls=%fused_computation.35 | loop fusion | flops 11009024 | bytes 5256192 | tf_op jit(solution)/shard_map/svf,svf->v/dot_general | solution.py:85
  53.7 14.7 %fusion.16 = (f32[256]{0:T(256)S(1)}, f32[256]{0:T(256)S(1)}, f32[256]{0:T(256)S(1)}, f32[256]{0:T(256)S(1)}, f32[256]{0:T(256)S(1)}, /*index=5*/f32[256]{0:T(25...) fusion(bf16[256,4,512]{2,1,0:T(4,128)(2,1)S(1)} %copy-done.1, pred[256]{0:T(512)(128)(4,1)S(1)} %get-tuple-element.76, ...), kind=kLoop, calls=%fused_computation.44 | loop fusion | flops 21493504 | bytes 10505472 | tf_op jit(solution)/shard_map/svf,svf->v/dot_general | solution.py:85
  68.4 9.0 %psum.7 = f32[256,13]{0,1:T(8,128)S(1)} all-reduce(f32[256,13]{0,1:T(8,128)S(1)} %stack.55), channel_id=1, replica_groups=mesh['vox'=16,'subj'=2] {'subj'}, use_global_device_ids=true, to_apply=%region_2.0 | all-reduce | flops 3328 | bytes 26624 | tf_op jit(solution)/shard_map/psum | solution.py:88
  77.4 1.0 fusion.61
  78.4 1.3 collective-permute-start.1
  79.7 9.9 %collective-permute-done.1 = f32[256]{0:T(256)S(1)} collective-permute-done((f32[256]{0:T(256)S(1)}, f32[256]{0:T(256)S(1)}, u32[]{:S(2)}, u32[]{:S(2)}) %collective-permute-start.1) | collective-permute-done | bytes 1056 | tf_op jit(solution)/shard_map/ppermute | solution.py:14
  89.6 7.0 %collective-permute-start.2 = (bf16[256,64]{0,1:T(8,128)(2,1)S(1)}, bf16[256,64]{0,1:T(8,128)(2,1)S(1)}, u32[]{:S(2)}, u32[]{:S(2)}) collective-permute-start(bf16[256,64]{0,1:T(8,128)(2,1)S(1)} %get-tuple-element.25), channel_id=1, source_target_pairs={{0,2},{2,4},{4,6},{6,8},{8,10},{10,12},{12,14},{14,16},{16,18},{18... | collective-permute-start | bytes 98312 | tf_op jit(solution)/shard_map/ppermute | solution.py:14
  97.1 1.3 collective-permute-start.3
  98.4 1.8 collective-permute-done.3
  101.0 3.1 %collective-permute-start.4 = (f32[64,64]{0,1:T(8,128)S(1)}, f32[64,64]{0,1:T(8,128)S(1)}, u32[]{:S(2)}, u32[]{:S(2)}) collective-permute-start(f32[64,64]{0,1:T(8,128)S(1)} %fusion.66), channel_id=1, source_target_pairs={{0,2},{2,0},{4,6},{6,4},{8,10},{10,8},{12,14},{14,12},{16,18},{18,... | collective-permute-start | bytes 49160 | tf_op jit(solution)/shard_map/ppermute | solution.py:19
  104.1 0.9 collective-permute-done.4
  105.0 1.6 collective-permute-start.6
  106.5 2.5 %collective-permute-start.7 = (f32[64,64]{0,1:T(8,128)S(1)}, f32[64,64]{0,1:T(8,128)S(1)}, u32[]{:S(2)}, u32[]{:S(2)}) collective-permute-start(f32[64,64]{0,1:T(8,128)S(1)} %add.178), channel_id=1, source_target_pairs={{0,12},{2,14},{4,8},{6,10},{8,4},{10,6},{12,0},{14,2},{16,28},{18,... | collective-permute-start | bytes 49160 | tf_op jit(solution)/shard_map/ppermute | solution.py:19
  109.1 2.2 %collective-permute-done.7 = f32[64,64]{0,1:T(8,128)S(1)} collective-permute-done((f32[64,64]{0,1:T(8,128)S(1)}, f32[64,64]{0,1:T(8,128)S(1)}, u32[]{:S(2)}, u32[]{:S(2)}) %collective-permute-start.7) | collective-permute-done | bytes 16416 | tf_op jit(solution)/shard_map/ppermute | solution.py:19
  111.4 1.6 collective-permute-done.5
  112.9 2.6 %collective-permute-start.8 = (f32[64,64]{0,1:T(8,128)S(1)}, f32[64,64]{0,1:T(8,128)S(1)}, u32[]{:S(2)}, u32[]{:S(2)}) collective-permute-start(f32[64,64]{0,1:T(8,128)S(1)} %add_add_fusion.2), channel_id=1, source_target_pairs={{0,16},{2,18},{4,20},{6,22},{8,24},{10,26},{12,28},{14,30},{16,0},... | collective-permute-start | bytes 49160 | tf_op jit(solution)/shard_map/ppermute | solution.py:19
  115.5 2.3 %collective-permute-done.8 = f32[64,64]{0,1:T(8,128)S(1)} collective-permute-done((f32[64,64]{0,1:T(8,128)S(1)}, f32[64,64]{0,1:T(8,128)S(1)}, u32[]{:S(2)}, u32[]{:S(2)}) %collective-permute-start.8) | collective-permute-done | bytes 16416 | tf_op jit(solution)/shard_map/ppermute | solution.py:19
  117.9 5.8 %cholesky.59 = f32[64,64]{1,0:T(8,128)S(1)} custom-call(f32[64,64]{1,0:T(8,128)S(1)} %fusion.49), custom_call_target="Cholesky" | custom-call | tf_op jit(solution)/shard_map/jit(cholesky)/cholesky | solution.py:52
  124.4 0.7 fusion.41
  125.1 4.9 %custom-call.7 = f32[1,64,64]{1,2,0:T(8,128)S(1)} custom-call(f32[1,64,64]{2,1,0:T(8,128)S(1)} %fusion.41), custom_call_target="InvertDiagBlocksLowerTriangular" | custom-call | tf_op jit(solution)/shard_map/triangular_solve/custom-call.0 | solution.py:53
  130.3 1.3 collective-permute-start.9
  132.1 1.6 collective-permute-start.10
  133.6 2.8 %collective-permute-done.10 = bf16[256,64]{0,1:T(8,128)(2,1)S(1)} collective-permute-done((bf16[256,64]{0,1:T(8,128)(2,1)S(1)}, bf16[256,64]{0,1:T(8,128)(2,1)S(1)}, u32[]{:S(2)}, u32[]{:S(2)}) %collective-permute-start.10) | collective-permute-done | bytes 32800 | tf_op jit(solution)/shard_map/ppermute | solution.py:14
  137.2 2.7 %collective-permute-start.11 = (f32[64,64]{0,1:T(8,128)S(1)}, f32[64,64]{0,1:T(8,128)S(1)}, u32[]{:S(2)}, u32[]{:S(2)}) collective-permute-start(f32[64,64]{0,1:T(8,128)S(1)} %fusion.68), channel_id=1, source_target_pairs={{0,2},{2,0},{4,6},{6,4},{8,10},{10,8},{12,14},{14,12},{16,18},{18,... | collective-permute-start | bytes 49160 | tf_op jit(solution)/shard_map/ppermute | solution.py:19
  139.9 0.9 collective-permute-done.11
  140.8 1.7 collective-permute-start.13
  142.5 2.7 %collective-permute-start.14 = (f32[64,64]{0,1:T(8,128)S(1)}, f32[64,64]{0,1:T(8,128)S(1)}, u32[]{:S(2)}, u32[]{:S(2)}) collective-permute-start(f32[64,64]{0,1:T(8,128)S(1)} %add.187), channel_id=1, source_target_pairs={{0,12},{2,14},{4,8},{6,10},{8,4},{10,6},{12,0},{14,2},{16,28},{18,... | collective-permute-start | bytes 49160 | tf_op jit(solution)/shard_map/ppermute | solution.py:19
  145.2 2.2 %collective-permute-done.14 = f32[64,64]{0,1:T(8,128)S(1)} collective-permute-done((f32[64,64]{0,1:T(8,128)S(1)}, f32[64,64]{0,1:T(8,128)S(1)}, u32[]{:S(2)}, u32[]{:S(2)}) %collective-permute-start.14) | collective-permute-done | bytes 16416 | tf_op jit(solution)/shard_map/ppermute | solution.py:19
  147.5 1.6 collective-permute-done.12
  149.1 1.1 collective-permute-start.15
  150.2 3.8 %collective-permute-done.15 = f32[64,64]{0,1:T(8,128)S(1)} collective-permute-done((f32[64,64]{0,1:T(8,128)S(1)}, f32[64,64]{0,1:T(8,128)S(1)}, u32[]{:S(2)}, u32[]{:S(2)}) %collective-permute-start.15) | collective-permute-done | bytes 16416 | tf_op jit(solution)/shard_map/ppermute | solution.py:19
  154.1 5.8 %cholesky.70 = f32[64,64]{1,0:T(8,128)S(1)} custom-call(f32[64,64]{1,0:T(8,128)S(1)} %fusion.47), custom_call_target="Cholesky" | custom-call | tf_op jit(solution)/shard_map/jit(cholesky)/cholesky | solution.py:52
  161.3 4.9 %custom-call.8 = f32[1,64,64]{1,2,0:T(8,128)S(1)} custom-call(f32[1,64,64]{2,1,0:T(8,128)S(1)} %fusion.42), custom_call_target="InvertDiagBlocksLowerTriangular" | custom-call | tf_op jit(solution)/shard_map/triangular_solve/custom-call.0 | solution.py:53
  166.4 1.3 collective-permute-start.16
  168.2 1.3 collective-permute-start.17
  169.5 3.0 %collective-permute-done.17 = bf16[256,64]{0,1:T(8,128)(2,1)S(1)} collective-permute-done((bf16[256,64]{0,1:T(8,128)(2,1)S(1)}, bf16[256,64]{0,1:T(8,128)(2,1)S(1)}, u32[]{:S(2)}, u32[]{:S(2)}) %collective-permute-start.17) | collective-permute-done | bytes 32800 | tf_op jit(solution)/shard_map/ppermute | solution.py:14
  173.4 2.7 %collective-permute-start.18 = (f32[64,64]{0,1:T(8,128)S(1)}, f32[64,64]{0,1:T(8,128)S(1)}, u32[]{:S(2)}, u32[]{:S(2)}) collective-permute-start(f32[64,64]{0,1:T(8,128)S(1)} %fusion.70), channel_id=1, source_target_pairs={{0,2},{2,0},{4,6},{6,4},{8,10},{10,8},{12,14},{14,12},{16,18},{18,... | collective-permute-start | bytes 49160 | tf_op jit(solution)/shard_map/ppermute | solution.py:19
  176.1 0.9 collective-permute-done.18
  176.9 1.7 collective-permute-start.20
  178.6 2.7 %collective-permute-start.21 = (f32[64,64]{0,1:T(8,128)S(1)}, f32[64,64]{0,1:T(8,128)S(1)}, u32[]{:S(2)}, u32[]{:S(2)}) collective-permute-start(f32[64,64]{0,1:T(8,128)S(1)} %add.196), channel_id=1, source_target_pairs={{0,12},{2,14},{4,8},{6,10},{8,4},{10,6},{12,0},{14,2},{16,28},{18,... | collective-permute-start | bytes 49160 | tf_op jit(solution)/shard_map/ppermute | solution.py:19
  181.3 2.3 %collective-permute-done.21 = f32[64,64]{0,1:T(8,128)S(1)} collective-permute-done((f32[64,64]{0,1:T(8,128)S(1)}, f32[64,64]{0,1:T(8,128)S(1)}, u32[]{:S(2)}, u32[]{:S(2)}) %collective-permute-start.21) | collective-permute-done | bytes 16416 | tf_op jit(solution)/shard_map/ppermute | solution.py:19
  183.6 1.6 collective-permute-done.19
  185.3 4.8 %collective-permute-done.22 = f32[64,64]{0,1:T(8,128)S(1)} collective-permute-done((f32[64,64]{0,1:T(8,128)S(1)}, f32[64,64]{0,1:T(8,128)S(1)}, u32[]{:S(2)}, u32[]{:S(2)}) %collective-permute-start.22) | collective-permute-done | bytes 16416 | tf_op jit(solution)/shard_map/ppermute | solution.py:19
  190.2 5.8 %cholesky.81 = f32[64,64]{1,0:T(8,128)S(1)} custom-call(f32[64,64]{1,0:T(8,128)S(1)} %fusion.45), custom_call_target="Cholesky" | custom-call | tf_op jit(solution)/shard_map/jit(cholesky)/cholesky | solution.py:52
  197.4 4.9 %custom-call.9 = f32[1,64,64]{1,2,0:T(8,128)S(1)} custom-call(f32[1,64,64]{2,1,0:T(8,128)S(1)} %fusion.43), custom_call_target="InvertDiagBlocksLowerTriangular" | custom-call | tf_op jit(solution)/shard_map/triangular_solve/custom-call.0 | solution.py:53
  202.3 0.9 convolution_bitcast_fusion
  (128 shorter events, 10.9 us)
Async XLA Ops:
  0.0 2.2 %copy-start = (bf16[4,256,512]{2,1,0:T(8,128)(2,1)S(1)}, bf16[4,256,512]{2,1,0:T(8,128)(2,1)}, u32[]{:S(2)}) copy-start(bf16[4,256,512]{2,1,0:T(8,128)(2,1)} %param.9) | copy-start | bytes 3145732
  2.1 5.5 %copy-start.7 = (s32[256,13]{0,1:T(8,128)S(1)}, s32[256,13]{0,1:T(8,128)}, u32[]{:S(2)}) copy-start(s32[256,13]{0,1:T(8,128)} %param.11) | copy-start | bytes 39940
  5.0 5.2 %collective-permute-start = (bf16[4,256,512]{2,0,1:T(4,128)(2,1)S(1)}, bf16[4,256,512]{2,0,1:T(4,128)(2,1)S(1)}, u32[]{:S(2)}, u32[]{:S(2)}) collective-permute-start(bf16[4,256,512]{2,0,1:T(4,128)(2,1)S(1)} %fusion.3), channel_id=1, source_target_pairs={{0,2},{2,4},{4,6},{6,8},{8,10},{10,12},{12,14},{14,16},{16,18},{18... | collective-permute-start | bytes 3145736 | tf_op jit(solution)/shard_map/ppermute | solution.py:14
  43.9 9.6 %copy-start.1 = (bf16[256,4,512]{2,1,0:T(4,128)(2,1)S(1)}, bf16[256,4,512]{2,1,0:T(4,128)(2,1)}, u32[]{:S(2)}) copy-start(bf16[256,4,512]{2,1,0:T(4,128)(2,1)} %gather_fusion.12) | copy-start | bytes 3145732
  43.9 9.6 %copy-start.2 = (bf16[256,4,512]{2,1,0:T(4,128)(2,1)S(1)}, bf16[256,4,512]{2,1,0:T(4,128)(2,1)}, u32[]{:S(2)}) copy-start(bf16[256,4,512]{2,1,0:T(4,128)(2,1)} %gather_fusion.11) | copy-start | bytes 3145732
  43.9 9.6 %copy-start.3 = (bf16[256,4,512]{2,1,0:T(4,128)(2,1)S(1)}, bf16[256,4,512]{2,1,0:T(4,128)(2,1)}, u32[]{:S(2)}) copy-start(bf16[256,4,512]{2,1,0:T(4,128)(2,1)} %gather_fusion.10) | copy-start | bytes 3145732
  43.9 9.6 %copy-start.4 = (bf16[256,4,512]{2,1,0:T(4,128)(2,1)S(1)}, bf16[256,4,512]{2,1,0:T(4,128)(2,1)}, u32[]{:S(2)}) copy-start(bf16[256,4,512]{2,1,0:T(4,128)(2,1)} %gather_fusion.9) | copy-start | bytes 3145732
  43.9 9.6 %copy-start.5 = (bf16[256,4,512]{2,1,0:T(4,128)(2,1)S(1)}, bf16[256,4,512]{2,1,0:T(4,128)(2,1)}, u32[]{:S(2)}) copy-start(bf16[256,4,512]{2,1,0:T(4,128)(2,1)} %gather_fusion.8) | copy-start | bytes 3145732
  44.0 9.6 %copy-start.9 = (pred[256]{0:T(512)(128)(4,1)S(1)}, pred[256]{0:T(512)(128)(4,1)}, u32[]{:S(2)}) copy-start(pred[256]{0:T(512)(128)(4,1)} %get-tuple-element.78) | copy-start | bytes 772
  44.0 9.6 %copy-start.10 = (pred[256]{0:T(512)(128)(4,1)S(1)}, pred[256]{0:T(512)(128)(4,1)}, u32[]{:S(2)}) copy-start(pred[256]{0:T(512)(128)(4,1)} %get-tuple-element.79) | copy-start | bytes 772
  44.0 9.6 %copy-start.11 = (pred[256]{0:T(512)(128)(4,1)S(1)}, pred[256]{0:T(512)(128)(4,1)}, u32[]{:S(2)}) copy-start(pred[256]{0:T(512)(128)(4,1)} %get-tuple-element.80) | copy-start | bytes 772
  44.0 9.6 %copy-start.12 = (pred[256]{0:T(512)(128)(4,1)S(1)}, pred[256]{0:T(512)(128)(4,1)}, u32[]{:S(2)}) copy-start(pred[256]{0:T(512)(128)(4,1)} %get-tuple-element.81) | copy-start | bytes 772
  44.0 9.6 %copy-start.13 = (pred[256]{0:T(512)(128)(4,1)S(1)}, pred[256]{0:T(512)(128)(4,1)}, u32[]{:S(2)}) copy-start(pred[256]{0:T(512)(128)(4,1)} %get-tuple-element.82) | copy-start | bytes 772
  44.0 9.6 %copy-start.14 = (pred[256]{0:T(512)(128)(4,1)S(1)}, pred[256]{0:T(512)(128)(4,1)}, u32[]{:S(2)}) copy-start(pred[256]{0:T(512)(128)(4,1)} %get-tuple-element.83) | copy-start | bytes 772
  44.0 9.6 %copy-start.15 = (pred[256]{0:T(512)(128)(4,1)S(1)}, pred[256]{0:T(512)(128)(4,1)}, u32[]{:S(2)}) copy-start(pred[256]{0:T(512)(128)(4,1)} %compare_and_fusion.8) | copy-start | bytes 772
  53.6 26.1 %copy-start.8 = (s32[256]{0:T(256)S(1)}, s32[256]{0:T(256)}, u32[]{:S(2)}) copy-start(s32[256]{0:T(256)} %param.10) | copy-start | bytes 3076
  53.6 36.0 %copy-start.6 = (f32[256,64]{0,1:T(8,128)S(1)}, f32[256,64]{0,1:T(8,128)}, u32[]{:S(2)}) copy-start(f32[256,64]{0,1:T(8,128)} %param.12) | copy-start | bytes 196612
  78.4 11.2 %collective-permute-start.1 = (f32[256]{0:T(256)S(1)}, f32[256]{0:T(256)S(1)}, u32[]{:S(2)}, u32[]{:S(2)}) collective-permute-start(f32[256]{0:T(256)S(1)} %slice.190), channel_id=1, source_target_pairs={{2,0},{4,2},{6,4},{8,6},{10,8},{12,10},{14,12},{16,14},{18,16},{20... | collective-permute-start | bytes 3080 | tf_op jit(solution)/shard_map/ppermute | solution.py:14
  89.6 8.8 %collective-permute-start.2 = (bf16[256,64]{0,1:T(8,128)(2,1)S(1)}, bf16[256,64]{0,1:T(8,128)(2,1)S(1)}, u32[]{:S(2)}, u32[]{:S(2)}) collective-permute-start(bf16[256,64]{0,1:T(8,128)(2,1)S(1)} %get-tuple-element.25), channel_id=1, source_target_pairs={{0,2},{2,4},{4,6},{6,8},{8,10},{10,12},{12,14},{14,16},{16,18},{18... | collective-permute-start | bytes 98312 | tf_op jit(solution)/shard_map/ppermute | solution.py:14
  97.1 3.1 %collective-permute-start.3 = (bf16[256,64]{0,1:T(8,128)(2,1)S(1)}, bf16[256,64]{0,1:T(8,128)(2,1)S(1)}, u32[]{:S(2)}, u32[]{:S(2)}) collective-permute-start(bf16[256,64]{0,1:T(8,128)(2,1)S(1)} %slice.264), channel_id=1, source_target_pairs={{2,0},{4,2},{6,4},{8,6},{10,8},{12,10},{14,12},{16,14},{18,16},{20... | collective-permute-start | bytes 98312 | tf_op jit(solution)/shard_map/ppermute | solution.py:14
  101.0 3.9 %collective-permute-start.4 = (f32[64,64]{0,1:T(8,128)S(1)}, f32[64,64]{0,1:T(8,128)S(1)}, u32[]{:S(2)}, u32[]{:S(2)}) collective-permute-start(f32[64,64]{0,1:T(8,128)S(1)} %fusion.66), channel_id=1, source_target_pairs={{0,2},{2,0},{4,6},{6,4},{8,10},{10,8},{12,14},{14,12},{16,18},{18,... | collective-permute-start | bytes 49160 | tf_op jit(solution)/shard_map/ppermute | solution.py:19
  105.0 4.1 %collective-permute-start.6 = (f32[64,64]{0,1:T(8,128)S(1)}, f32[64,64]{0,1:T(8,128)S(1)}, u32[]{:S(2)}, u32[]{:S(2)}) collective-permute-start(f32[64,64]{0,1:T(8,128)S(1)} %add.178), channel_id=1, source_target_pairs={{0,8},{2,10},{4,12},{6,14},{8,0},{10,2},{12,4},{14,6},{16,24},{18,... | collective-permute-start | bytes 49160 | tf_op jit(solution)/shard_map/ppermute | solution.py:19
  106.5 4.8 %collective-permute-start.7 = (f32[64,64]{0,1:T(8,128)S(1)}, f32[64,64]{0,1:T(8,128)S(1)}, u32[]{:S(2)}, u32[]{:S(2)}) collective-permute-start(f32[64,64]{0,1:T(8,128)S(1)} %add.178), channel_id=1, source_target_pairs={{0,12},{2,14},{4,8},{6,10},{8,4},{10,6},{12,0},{14,2},{16,28},{18,... | collective-permute-start | bytes 49160 | tf_op jit(solution)/shard_map/ppermute | solution.py:19
  109.0 3.9 %collective-permute-start.5 = (f32[64,64]{0,1:T(8,128)S(1)}, f32[64,64]{0,1:T(8,128)S(1)}, u32[]{:S(2)}, u32[]{:S(2)}) collective-permute-start(f32[64,64]{0,1:T(8,128)S(1)} %add.178), channel_id=1, source_target_pairs={{0,4},{2,6},{4,0},{6,2},{8,12},{10,14},{12,8},{14,10},{16,20},{18,... | collective-permute-start | bytes 49160 | tf_op jit(solution)/shard_map/ppermute | solution.py:19
  112.9 4.9 %collective-permute-start.8 = (f32[64,64]{0,1:T(8,128)S(1)}, f32[64,64]{0,1:T(8,128)S(1)}, u32[]{:S(2)}, u32[]{:S(2)}) collective-permute-start(f32[64,64]{0,1:T(8,128)S(1)} %add_add_fusion.2), channel_id=1, source_target_pairs={{0,16},{2,18},{4,20},{6,22},{8,24},{10,26},{12,28},{14,30},{16,0},... | collective-permute-start | bytes 49160 | tf_op jit(solution)/shard_map/ppermute | solution.py:19
  130.3 3.3 %collective-permute-start.9 = (bf16[256,64]{0,1:T(8,128)(2,1)S(1)}, bf16[256,64]{0,1:T(8,128)(2,1)S(1)}, u32[]{:S(2)}, u32[]{:S(2)}) collective-permute-start(bf16[256,64]{0,1:T(8,128)(2,1)S(1)} %get-tuple-element.23), channel_id=1, source_target_pairs={{0,2},{2,4},{4,6},{6,8},{8,10},{10,12},{12,14},{14,16},{16,18},{18... | collective-permute-start | bytes 98312 | tf_op jit(solution)/shard_map/ppermute | solution.py:14
  132.1 4.3 %collective-permute-start.10 = (bf16[256,64]{0,1:T(8,128)(2,1)S(1)}, bf16[256,64]{0,1:T(8,128)(2,1)S(1)}, u32[]{:S(2)}, u32[]{:S(2)}) collective-permute-start(bf16[256,64]{0,1:T(8,128)(2,1)S(1)} %slice.263), channel_id=1, source_target_pairs={{2,0},{4,2},{6,4},{8,6},{10,8},{12,10},{14,12},{16,14},{18,16},{20... | collective-permute-start | bytes 98312 | tf_op jit(solution)/shard_map/ppermute | solution.py:14
  137.2 3.6 %collective-permute-start.11 = (f32[64,64]{0,1:T(8,128)S(1)}, f32[64,64]{0,1:T(8,128)S(1)}, u32[]{:S(2)}, u32[]{:S(2)}) collective-permute-start(f32[64,64]{0,1:T(8,128)S(1)} %fusion.68), channel_id=1, source_target_pairs={{0,2},{2,0},{4,6},{6,4},{8,10},{10,8},{12,14},{14,12},{16,18},{18,... | collective-permute-start | bytes 49160 | tf_op jit(solution)/shard_map/ppermute | solution.py:19
  140.8 4.4 %collective-permute-start.13 = (f32[64,64]{0,1:T(8,128)S(1)}, f32[64,64]{0,1:T(8,128)S(1)}, u32[]{:S(2)}, u32[]{:S(2)}) collective-permute-start(f32[64,64]{0,1:T(8,128)S(1)} %add.187), channel_id=1, source_target_pairs={{0,8},{2,10},{4,12},{6,14},{8,0},{10,2},{12,4},{14,6},{16,24},{18,... | collective-permute-start | bytes 49160 | tf_op jit(solution)/shard_map/ppermute | solution.py:19
  142.5 5.0 %collective-permute-start.14 = (f32[64,64]{0,1:T(8,128)S(1)}, f32[64,64]{0,1:T(8,128)S(1)}, u32[]{:S(2)}, u32[]{:S(2)}) collective-permute-start(f32[64,64]{0,1:T(8,128)S(1)} %add.187), channel_id=1, source_target_pairs={{0,12},{2,14},{4,8},{6,10},{8,4},{10,6},{12,0},{14,2},{16,28},{18,... | collective-permute-start | bytes 49160 | tf_op jit(solution)/shard_map/ppermute | solution.py:19
  145.2 3.9 %collective-permute-start.12 = (f32[64,64]{0,1:T(8,128)S(1)}, f32[64,64]{0,1:T(8,128)S(1)}, u32[]{:S(2)}, u32[]{:S(2)}) collective-permute-start(f32[64,64]{0,1:T(8,128)S(1)} %add.187), channel_id=1, source_target_pairs={{0,4},{2,6},{4,0},{6,2},{8,12},{10,14},{12,8},{14,10},{16,20},{18,... | collective-permute-start | bytes 49160 | tf_op jit(solution)/shard_map/ppermute | solution.py:19
  149.1 4.9 %collective-permute-start.15 = (f32[64,64]{0,1:T(8,128)S(1)}, f32[64,64]{0,1:T(8,128)S(1)}, u32[]{:S(2)}, u32[]{:S(2)}) collective-permute-start(f32[64,64]{0,1:T(8,128)S(1)} %add_add_fusion.1), channel_id=1, source_target_pairs={{0,16},{2,18},{4,20},{6,22},{8,24},{10,26},{12,28},{14,30},{16,0},... | collective-permute-start | bytes 49160 | tf_op jit(solution)/shard_map/ppermute | solution.py:19
  166.4 3.1 %collective-permute-start.16 = (bf16[256,64]{0,1:T(8,128)(2,1)S(1)}, bf16[256,64]{0,1:T(8,128)(2,1)S(1)}, u32[]{:S(2)}, u32[]{:S(2)}) collective-permute-start(bf16[256,64]{0,1:T(8,128)(2,1)S(1)} %get-tuple-element.21), channel_id=1, source_target_pairs={{0,2},{2,4},{4,6},{6,8},{8,10},{10,12},{12,14},{14,16},{16,18},{18... | collective-permute-start | bytes 98312 | tf_op jit(solution)/shard_map/ppermute | solution.py:14
  168.2 4.3 %collective-permute-start.17 = (bf16[256,64]{0,1:T(8,128)(2,1)S(1)}, bf16[256,64]{0,1:T(8,128)(2,1)S(1)}, u32[]{:S(2)}, u32[]{:S(2)}) collective-permute-start(bf16[256,64]{0,1:T(8,128)(2,1)S(1)} %slice.262), channel_id=1, source_target_pairs={{2,0},{4,2},{6,4},{8,6},{10,8},{12,10},{14,12},{16,14},{18,16},{20... | collective-permute-start | bytes 98312 | tf_op jit(solution)/shard_map/ppermute | solution.py:14
  173.4 3.6 %collective-permute-start.18 = (f32[64,64]{0,1:T(8,128)S(1)}, f32[64,64]{0,1:T(8,128)S(1)}, u32[]{:S(2)}, u32[]{:S(2)}) collective-permute-start(f32[64,64]{0,1:T(8,128)S(1)} %fusion.70), channel_id=1, source_target_pairs={{0,2},{2,0},{4,6},{6,4},{8,10},{10,8},{12,14},{14,12},{16,18},{18,... | collective-permute-start | bytes 49160 | tf_op jit(solution)/shard_map/ppermute | solution.py:19
  176.9 4.4 %collective-permute-start.20 = (f32[64,64]{0,1:T(8,128)S(1)}, f32[64,64]{0,1:T(8,128)S(1)}, u32[]{:S(2)}, u32[]{:S(2)}) collective-permute-start(f32[64,64]{0,1:T(8,128)S(1)} %add.196), channel_id=1, source_target_pairs={{0,8},{2,10},{4,12},{6,14},{8,0},{10,2},{12,4},{14,6},{16,24},{18,... | collective-permute-start | bytes 49160 | tf_op jit(solution)/shard_map/ppermute | solution.py:19
  178.6 5.0 %collective-permute-start.21 = (f32[64,64]{0,1:T(8,128)S(1)}, f32[64,64]{0,1:T(8,128)S(1)}, u32[]{:S(2)}, u32[]{:S(2)}) collective-permute-start(f32[64,64]{0,1:T(8,128)S(1)} %add.196), channel_id=1, source_target_pairs={{0,12},{2,14},{4,8},{6,10},{8,4},{10,6},{12,0},{14,2},{16,28},{18,... | collective-permute-start | bytes 49160 | tf_op jit(solution)/shard_map/ppermute | solution.py:19
  181.3 3.9 %collective-permute-start.19 = (f32[64,64]{0,1:T(8,128)S(1)}, f32[64,64]{0,1:T(8,128)S(1)}, u32[]{:S(2)}, u32[]{:S(2)}) collective-permute-start(f32[64,64]{0,1:T(8,128)S(1)} %add.196), channel_id=1, source_target_pairs={{0,4},{2,6},{4,0},{6,2},{8,12},{10,14},{12,8},{14,10},{16,20},{18,... | collective-permute-start | bytes 49160 | tf_op jit(solution)/shard_map/ppermute | solution.py:19
  185.2 4.9 %collective-permute-start.22 = (f32[64,64]{0,1:T(8,128)S(1)}, f32[64,64]{0,1:T(8,128)S(1)}, u32[]{:S(2)}, u32[]{:S(2)}) collective-permute-start(f32[64,64]{0,1:T(8,128)S(1)} %add_add_fusion), channel_id=1, source_target_pairs={{0,16},{2,18},{4,20},{6,22},{8,24},{10,26},{12,28},{14,30},{16,0},... | collective-permute-start | bytes 49160 | tf_op jit(solution)/shard_map/ppermute | solution.py:19
